TPU v7x, 32 devices: a whole 2x2x4 slice. The times are simulated.
32 devices in a mesh: gx: 4 (over y, x), gy: 4 (over z), gz: 2 (over core).
Axes of the slice: x: 2, y: 2, z: 4, core: 2. Of those that a mesh axis runs over, the one named last changes fastest.
Arguments:
- blocks: int32 [32768, 4], P(('gx', 'gy', 'gz')), may hold values from 0 to 15, as said below
- coefficients: bfloat16 [32768, 4, 128], P(('gx', 'gy', 'gz')), may hold values from -80 to 80
- residuals: float32 [32768], P(('gx', 'gy', 'gz')), may hold values from -3000 to 3000
Outputs:
- factor: float32 [4, 4, 128, 4, 4, 128], P('gx', None, None, 'gy')
- solution: float32 [16, 128], replicated
Inputs may be any that keep to these rules, and one draw needn't show every extreme that they name: Each row names 4 different blocks.
All inputs are finite; a program needn't handle non-finite values.
Results may differ from a plain program's by a relative error of at most 0.0003.
Values sent between devices are 32-bit elements; how exact they have to be, the bound alone decides.
A program may use at most 128 MiB of HBM per device.

v0:
```python
import jax
import jax.numpy as jnp
from jax import lax
from jax.sharding import PartitionSpec as P

G = 2048
BS = 128


def from_root(block, axis, source):
    block = jnp.where(lax.axis_index(axis) == source, block, jnp.zeros_like(block))
    return lax.psum(block, axis)


def on_device(blocks, coefficients, residuals):
    row_count = lax.axis_size("gx")
    col_count = lax.axis_size("gy")
    row_index = lax.axis_index("gx")
    col_index = lax.axis_index("gy")
    scale = 1.0 / (coefficients.shape[0] * row_count * col_count * lax.axis_size("gz"))
    width = coefficients.shape[2]
    nblock = G // BS
    per_dev = nblock // row_count
    target = (
        jnp.arange(per_dev, dtype=jnp.int32)[None, :] * row_count
        + jnp.arange(row_count, dtype=jnp.int32)[:, None]
    ).reshape(-1)
    placed = (blocks[:, :, None] == target[None, None, :]).astype(jnp.bfloat16)
    design = jnp.einsum("osz,osx->ozx", placed, coefficients, preferred_element_type=jnp.float32)
    design = design.astype(jnp.bfloat16).reshape(-1, row_count, per_dev, width)
    natural = (blocks[:, :, None] == jnp.arange(nblock, dtype=jnp.int32)[None, None, :]).astype(
        jnp.float32
    )
    weighted = coefficients.astype(jnp.float32) * residuals[:, None, None]
    rhs_local = (
        jnp.einsum("osb,osx->bx", natural, weighted, precision=lax.Precision.HIGHEST) * scale
    )
    rhs = lax.psum(rhs_local, ("gx", "gy", "gz"))
    term = (
        jnp.einsum("opix,oqjy->pqixjy", design, design, preferred_element_type=jnp.float32) * scale
    )
    term = term.reshape(row_count * col_count, per_dev, width, per_dev, width)
    halves = lax.psum_scatter(term, "gz", scatter_dimension=2, tiled=True)
    halves = lax.psum_scatter(halves, ("gx", "gy"), scatter_dimension=0, tiled=True)
    summed = lax.all_gather(halves, "gz", axis=2, tiled=True)
    matrix = summed.reshape(per_dev, width, per_dev, width)
    zero = jnp.zeros((), jnp.int32)
    block_ids = (
        jnp.arange(per_dev, dtype=jnp.int32)[None, :] * row_count
        + jnp.arange(row_count, dtype=jnp.int32)[:, None]
    )

    def factor_step(step, state):
        working, factor, pivots = state
        step_row = step % row_count
        step_local_row = step // row_count
        step_col = step % col_count
        step_local_col = step // col_count
        column = lax.dynamic_slice(
            working, (zero, zero, step_local_col, zero), (per_dev, width, 1, width)
        ).reshape(per_dev, width, width)
        row_raw = from_root(column, "gy", step_col)
        whole = lax.all_gather(row_raw, "gx", axis=0, tiled=True).reshape(
            row_count, per_dev, width, width
        )
        own_diag = lax.dynamic_slice(
            whole, (step_row, step_local_row, zero, zero), (1, 1, width, width)
        ).reshape(width, width)
        chol = jnp.linalg.cholesky(own_diag)
        stacked = whole.transpose(3, 0, 1, 2).reshape(width, row_count * per_dev * width)
        solved = jax.scipy.linalg.solve_triangular(chol, stacked, lower=True)
        panel_all = solved.reshape(width, row_count, per_dev, width).transpose(1, 2, 3, 0)
        panel_all = jnp.where((block_ids > step)[:, :, None, None], panel_all, 0.0)
        row_panel = lax.dynamic_index_in_dim(panel_all, row_index, 0, keepdims=False)
        col_panel = lax.dynamic_index_in_dim(panel_all, col_index, 0, keepdims=False)
        working = working - jnp.einsum(
            "rxk,cyk->rxcy", row_panel, col_panel, precision=lax.Precision.HIGHEST
        )
        on_diag = (jnp.arange(per_dev, dtype=jnp.int32) == step_local_row) & (row_index == step_row)
        new_column = row_panel + jnp.where(on_diag[:, None, None], chol[None], 0.0)
        old_column = lax.dynamic_slice(
            factor, (zero, zero, step_local_col, zero), (per_dev, width, 1, width)
        ).reshape(per_dev, width, width)
        kept = jnp.where(col_index == step_col, new_column, old_column)
        factor = lax.dynamic_update_slice(
            factor, kept.reshape(per_dev, width, 1, width), (zero, zero, step_local_col, zero)
        )
        pivots = lax.dynamic_update_slice(pivots, chol[None], (step, zero, zero))
        return (working, factor, pivots)

    start_state = (matrix, jnp.zeros_like(matrix), jnp.zeros((nblock, width, width), jnp.float32))
    _, factor, pivots = lax.fori_loop(0, nblock, factor_step, start_state)
    shaped = factor.reshape(1, per_dev, width, 1, per_dev, width)
    across = lax.all_gather(shaped, "gy", axis=3, tiled=True)
    whole = lax.all_gather(across, "gx", axis=0, tiled=True)
    lower = whole.transpose(1, 0, 2, 4, 3, 5).reshape(nblock * width, nblock * width)
    middle = jax.scipy.linalg.solve_triangular(lower, rhs.reshape(-1), lower=True)
    answer = jax.scipy.linalg.solve_triangular(lower, middle, lower=True, trans=1)
    solution = answer.reshape(nblock, width)
    return (factor.reshape(1, per_dev, width, 1, per_dev, width), solution)


def solution(mesh):
    in_specs = (
        P(("gx", "gy", "gz"), None),
        P(("gx", "gy", "gz"), None, None),
        P(("gx", "gy", "gz")),
    )
    out_specs = (P("gx", None, None, "gy", None, None), P())
    return jax.shard_map(
        on_device, mesh=mesh, in_specs=in_specs, out_specs=out_specs, check_vma=False
    )
```

profile of v0, /device:TPU:0, one launch (start us, length us, event | category | flops | bytes accessed | tf_op | source)
XLA Modules:
  0.0 2390.0 jit_solution(993266467958038092)
XLA Ops:
  72.9 183.3 %reduce-scatter.5.cloned.1.call-done = f32[1,4,64,4,128]{4,2,3,1,0:T(8,128)} async-done(((f32[16,4,64,4,128]{4,2,3,1,0:T(8,128)}), f32[1,4,64,4,128]{4,2,3,1,0:T(8,128)}) %reduce-scatter.5.cloned.1.call-update) | async-done | bytes 524304 | tf_op jit(solution)/shard_map/reduce_scatter | solution.py:44
  266.6 1563.2 %while.20 = (s32[]{:T(128)}, f32[4,128,4,128]{3,1,2,0:T(8,128)}, f32[4,128,4,128]{3,1,2,0:T(8,128)S(1)}, s32[]{:T(128)}, s32[]{:T(128)}, /*index=5*/s32[]{:T(128...) while((s32[]{:T(128)}, f32[4,128,4,128]{3,1,2,0:T(8,128)}, ...), condition=%wide.region_6.7_spmd.clone, body=%wide.region_2.6_spmd.clone.sunk | while | flops 806305984 | bytes 14485572 | solution.py:92
  268.5 38.3 %all-reduce.2.cloned.1.call-done = f32[4,128,128]{2,1,0:T(8,128)} async-done(((f32[4,128,128]{2,1,0:T(8,128)}), f32[4,128,128]{2,1,0:T(8,128)}) %all-reduce.2.cloned.1.call-update) | async-done | bytes 262160 | tf_op jit(solution)/shard_map/while/body/eval_jaxpr/psum | solution.py:12
  367.0 37.2 %all-reduce.2.cloned.1.call-done = f32[4,128,128]{2,1,0:T(8,128)} async-done(((f32[4,128,128]{2,1,0:T(8,128)}), f32[4,128,128]{2,1,0:T(8,128)}) %all-reduce.2.cloned.1.call-update) | async-done | bytes 262160 | tf_op jit(solution)/shard_map/while/body/eval_jaxpr/psum | solution.py:12
  464.6 37.5 %all-reduce.2.cloned.1.call-done = f32[4,128,128]{2,1,0:T(8,128)} async-done(((f32[4,128,128]{2,1,0:T(8,128)}), f32[4,128,128]{2,1,0:T(8,128)}) %all-reduce.2.cloned.1.call-update) | async-done | bytes 262160 | tf_op jit(solution)/shard_map/while/body/eval_jaxpr/psum | solution.py:12
  562.5 37.2 %all-reduce.2.cloned.1.call-done = f32[4,128,128]{2,1,0:T(8,128)} async-done(((f32[4,128,128]{2,1,0:T(8,128)}), f32[4,128,128]{2,1,0:T(8,128)}) %all-reduce.2.cloned.1.call-update) | async-done | bytes 262160 | tf_op jit(solution)/shard_map/while/body/eval_jaxpr/psum | solution.py:12
  599.8 28.1 %all-gather.12.cloned.1.call-done = f32[16,128,128]{2,1,0:T(8,128)} async-done(((f32[4,128,128]{2,1,0:T(8,128)}), f32[16,128,128]{2,1,0:T(8,128)}) %all-gather.12.cloned.1.call-update) | async-done | bytes 1048592 | tf_op jit(solution)/shard_map/while/body/eval_jaxpr/all_gather | solution.py:63
  660.0 37.2 %all-reduce.2.cloned.1.call-done = f32[4,128,128]{2,1,0:T(8,128)} async-done(((f32[4,128,128]{2,1,0:T(8,128)}), f32[4,128,128]{2,1,0:T(8,128)}) %all-reduce.2.cloned.1.call-update) | async-done | bytes 262160 | tf_op jit(solution)/shard_map/while/body/eval_jaxpr/psum | solution.py:12
  757.6 37.2 %all-reduce.2.cloned.1.call-done = f32[4,128,128]{2,1,0:T(8,128)} async-done(((f32[4,128,128]{2,1,0:T(8,128)}), f32[4,128,128]{2,1,0:T(8,128)}) %all-reduce.2.cloned.1.call-update) | async-done | bytes 262160 | tf_op jit(solution)/shard_map/while/body/eval_jaxpr/psum | solution.py:12
  855.0 37.2 %all-reduce.2.cloned.1.call-done = f32[4,128,128]{2,1,0:T(8,128)} async-done(((f32[4,128,128]{2,1,0:T(8,128)}), f32[4,128,128]{2,1,0:T(8,128)}) %all-reduce.2.cloned.1.call-update) | async-done | bytes 262160 | tf_op jit(solution)/shard_map/while/body/eval_jaxpr/psum | solution.py:12
  952.5 37.2 %all-reduce.2.cloned.1.call-done = f32[4,128,128]{2,1,0:T(8,128)} async-done(((f32[4,128,128]{2,1,0:T(8,128)}), f32[4,128,128]{2,1,0:T(8,128)}) %all-reduce.2.cloned.1.call-update) | async-done | bytes 262160 | tf_op jit(solution)/shard_map/while/body/eval_jaxpr/psum | solution.py:12
  1050.0 37.2 %all-reduce.2.cloned.1.call-done = f32[4,128,128]{2,1,0:T(8,128)} async-done(((f32[4,128,128]{2,1,0:T(8,128)}), f32[4,128,128]{2,1,0:T(8,128)}) %all-reduce.2.cloned.1.call-update) | async-done | bytes 262160 | tf_op jit(solution)/shard_map/while/body/eval_jaxpr/psum | solution.py:12
  1147.6 37.5 %all-reduce.2.cloned.1.call-done = f32[4,128,128]{2,1,0:T(8,128)} async-done(((f32[4,128,128]{2,1,0:T(8,128)}), f32[4,128,128]{2,1,0:T(8,128)}) %all-reduce.2.cloned.1.call-update) | async-done | bytes 262160 | tf_op jit(solution)/shard_map/while/body/eval_jaxpr/psum | solution.py:12
  1245.5 37.2 %all-reduce.2.cloned.1.call-done = f32[4,128,128]{2,1,0:T(8,128)} async-done(((f32[4,128,128]{2,1,0:T(8,128)}), f32[4,128,128]{2,1,0:T(8,128)}) %all-reduce.2.cloned.1.call-update) | async-done | bytes 262160 | tf_op jit(solution)/shard_map/while/body/eval_jaxpr/psum | solution.py:12
  1343.1 37.2 %all-reduce.2.cloned.1.call-done = f32[4,128,128]{2,1,0:T(8,128)} async-done(((f32[4,128,128]{2,1,0:T(8,128)}), f32[4,128,128]{2,1,0:T(8,128)}) %all-reduce.2.cloned.1.call-update) | async-done | bytes 262160 | tf_op jit(solution)/shard_map/while/body/eval_jaxpr/psum | solution.py:12
  1440.5 37.5 %all-reduce.2.cloned.1.call-done = f32[4,128,128]{2,1,0:T(8,128)} async-done(((f32[4,128,128]{2,1,0:T(8,128)}), f32[4,128,128]{2,1,0:T(8,128)}) %all-reduce.2.cloned.1.call-update) | async-done | bytes 262160 | tf_op jit(solution)/shard_map/while/body/eval_jaxpr/psum | solution.py:12
  1538.4 37.2 %all-reduce.2.cloned.1.call-done = f32[4,128,128]{2,1,0:T(8,128)} async-done(((f32[4,128,128]{2,1,0:T(8,128)}), f32[4,128,128]{2,1,0:T(8,128)}) %all-reduce.2.cloned.1.call-update) | async-done | bytes 262160 | tf_op jit(solution)/shard_map/while/body/eval_jaxpr/psum | solution.py:12
  1636.0 37.5 %all-reduce.2.cloned.1.call-done = f32[4,128,128]{2,1,0:T(8,128)} async-done(((f32[4,128,128]{2,1,0:T(8,128)}), f32[4,128,128]{2,1,0:T(8,128)}) %all-reduce.2.cloned.1.call-update) | async-done | bytes 262160 | tf_op jit(solution)/shard_map/while/body/eval_jaxpr/psum | solution.py:12
  1733.7 37.5 %all-reduce.2.cloned.1.call-done = f32[4,128,128]{2,1,0:T(8,128)} async-done(((f32[4,128,128]{2,1,0:T(8,128)}), f32[4,128,128]{2,1,0:T(8,128)}) %all-reduce.2.cloned.1.call-update) | async-done | bytes 262160 | tf_op jit(solution)/shard_map/while/body/eval_jaxpr/psum | solution.py:12
  1830.9 81.8 %all-gather.10.cloned.1.call-done = f32[4,128,16,128]{3,1,2,0:T(8,128)} async-done(((f32[4,128,4,128]{3,1,2,0:T(8,128)}), f32[4,128,16,128]{3,1,2,0:T(8,128)}) %all-gather.10.cloned.1.call-update) | async-done | bytes 4194320 | tf_op jit(solution)/shard_map/all_gather | solution.py:94
  1916.5 39.8 %psum.21 = f32[16,128]{1,0:T(8,128)S(1)} all-reduce(f32[16,128]{1,0:T(8,128)S(1)} %fusion.18), channel_id=1, replica_groups=mesh['gx'=4,'gy'=4,'gz'=2] {'gx','gy','gz'}, use_global_device_ids=true, to_apply=%region_7.8 | all-reduce | flops 2048 | bytes 16384 | tf_op jit(solution)/shard_map/psum | solution.py:38
  1959.2 111.7 %all-gather.8.cloned.1.call-done = f32[4,4,128,4,4,128]{5,2,4,3,1,0:T(8,128)} async-done(((f32[1,4,128,4,4,128]{5,2,4,3,1,0:T(8,128)}), f32[4,4,128,4,4,128]{5,2,4,3,1,0:T(8,128)}) %all-gather.8.cloned.1.call-update) | async-done | bytes 16777232 | tf_op jit(solution)/shard_map/all_gather | solution.py:95
  2124.2 47.6 %while.19 = (s32[]{:T(128)}, f32[2048,2048]{1,0:T(8,128)}, s32[16,2]{0,1:T(2,128)S(1)}, f32[16,128,128]{2,1,0:T(8,128)S(1)}, s32[]{:T(128)}) while((s32[]{:T(128)}, f32[2048,2048]{1,0:T(8,128)}, s32[16,2]{0,1:T(2,128)S(1)}, f32[16,128,128]{2,1,0:T(8,128)S(1)}, s32[]{:T(128)}) %tuple.184), condition=%wide.while_cond, body=%wide.while_body.sunk | while | flops 2 | bytes 131181 | solution.py:98
  2171.8 157.4 %custom-call.28 = f32[16,128,128]{1,2,0:T(8,128)S(1)} custom-call(f32[16,128,128]{2,1,0:T(8,128)S(1)} %get-tuple-element.183), custom_call_target="InvertDiagBlocksLowerTriangular" | custom-call | tf_op jit(solution)/shard_map/jit(_solve_triangular)/triangular_solve | solution.py:98
  (583 shorter events, 1172.5 us)
Async XLA Ops:
  7.2 65.2 %reduce-scatter.3.cloned.1.call-start = ((), (), s32[]{:S(2)}) async-start(), calls=%async_computation.2 | async-start | bytes 25165824 | tf_op jit(solution)/shard_map/reduce_scatter | solution.py:43
  44.5 211.7 %reduce-scatter.5.cloned.1.call-start = ((), (), s32[]{:S(2)}) async-start(), calls=%async_computation.3 | async-start | bytes 8912896 | tf_op jit(solution)/shard_map/reduce_scatter | solution.py:44
  72.4 194.0 %all-gather.6.cloned.1.call-start = ((), (), s32[]{:S(2)}) async-start(), calls=%async_computation.4 | async-start | bytes 1572864 | tf_op jit(solution)/shard_map/all_gather | solution.py:45
  266.6 40.2 %all-reduce.2.cloned.1.call-start = ((), (), s32[]{:S(2)}) async-start(), calls=%async_computation.7 | async-start | bytes 524288 | tf_op jit(solution)/shard_map/while/body/eval_jaxpr/psum | solution.py:12
  268.4 66.4 %all-gather.12.cloned.1.call-start = ((), (), s32[]{:S(2)}) async-start(), calls=%async_computation.8 | async-start | bytes 1310720 | tf_op jit(solution)/shard_map/while/body/eval_jaxpr/all_gather | solution.py:63
  366.9 65.5 %all-gather.12.cloned.1.call-start = ((), (), s32[]{:S(2)}) async-start(), calls=%async_computation.8 | async-start | bytes 1310720 | tf_op jit(solution)/shard_map/while/body/eval_jaxpr/all_gather | solution.py:63
  464.5 65.8 %all-gather.12.cloned.1.call-start = ((), (), s32[]{:S(2)}) async-start(), calls=%async_computation.8 | async-start | bytes 1310720 | tf_op jit(solution)/shard_map/while/body/eval_jaxpr/all_gather | solution.py:63
  562.4 65.5 %all-gather.12.cloned.1.call-start = ((), (), s32[]{:S(2)}) async-start(), calls=%async_computation.8 | async-start | bytes 1310720 | tf_op jit(solution)/shard_map/while/body/eval_jaxpr/all_gather | solution.py:63
  660.0 65.5 %all-gather.12.cloned.1.call-start = ((), (), s32[]{:S(2)}) async-start(), calls=%async_computation.8 | async-start | bytes 1310720 | tf_op jit(solution)/shard_map/while/body/eval_jaxpr/all_gather | solution.py:63
  757.6 65.3 %all-gather.12.cloned.1.call-start = ((), (), s32[]{:S(2)}) async-start(), calls=%async_computation.8 | async-start | bytes 1310720 | tf_op jit(solution)/shard_map/while/body/eval_jaxpr/all_gather | solution.py:63
  855.0 65.3 %all-gather.12.cloned.1.call-start = ((), (), s32[]{:S(2)}) async-start(), calls=%async_computation.8 | async-start | bytes 1310720 | tf_op jit(solution)/shard_map/while/body/eval_jaxpr/all_gather | solution.py:63
  952.4 65.5 %all-gather.12.cloned.1.call-start = ((), (), s32[]{:S(2)}) async-start(), calls=%async_computation.8 | async-start | bytes 1310720 | tf_op jit(solution)/shard_map/while/body/eval_jaxpr/all_gather | solution.py:63
  1050.0 65.5 %all-gather.12.cloned.1.call-start = ((), (), s32[]{:S(2)}) async-start(), calls=%async_computation.8 | async-start | bytes 1310720 | tf_op jit(solution)/shard_map/while/body/eval_jaxpr/all_gather | solution.py:63
  1147.6 65.8 %all-gather.12.cloned.1.call-start = ((), (), s32[]{:S(2)}) async-start(), calls=%async_computation.8 | async-start | bytes 1310720 | tf_op jit(solution)/shard_map/while/body/eval_jaxpr/all_gather | solution.py:63
  1245.5 65.5 %all-gather.12.cloned.1.call-start = ((), (), s32[]{:S(2)}) async-start(), calls=%async_computation.8 | async-start | bytes 1310720 | tf_op jit(solution)/shard_map/while/body/eval_jaxpr/all_gather | solution.py:63
  1343.1 65.3 %all-gather.12.cloned.1.call-start = ((), (), s32[]{:S(2)}) async-start(), calls=%async_computation.8 | async-start | bytes 1310720 | tf_op jit(solution)/shard_map/while/body/eval_jaxpr/all_gather | solution.py:63
  1438.7 39.3 %all-reduce.2.cloned.1.call-start = ((), (), s32[]{:S(2)}) async-start(), calls=%async_computation.7 | async-start | bytes 524288 | tf_op jit(solution)/shard_map/while/body/eval_jaxpr/psum | solution.py:12
  1440.5 65.8 %all-gather.12.cloned.1.call-start = ((), (), s32[]{:S(2)}) async-start(), calls=%async_computation.8 | async-start | bytes 1310720 | tf_op jit(solution)/shard_map/while/body/eval_jaxpr/all_gather | solution.py:63
  1538.4 65.5 %all-gather.12.cloned.1.call-start = ((), (), s32[]{:S(2)}) async-start(), calls=%async_computation.8 | async-start | bytes 1310720 | tf_op jit(solution)/shard_map/while/body/eval_jaxpr/all_gather | solution.py:63
  1636.0 65.7 %all-gather.12.cloned.1.call-start = ((), (), s32[]{:S(2)}) async-start(), calls=%async_computation.8 | async-start | bytes 1310720 | tf_op jit(solution)/shard_map/while/body/eval_jaxpr/all_gather | solution.py:63
  1731.9 39.4 %all-reduce.2.cloned.1.call-start = ((), (), s32[]{:S(2)}) async-start(), calls=%async_computation.7 | async-start | bytes 524288 | tf_op jit(solution)/shard_map/while/body/eval_jaxpr/psum | solution.py:12
  1733.7 65.8 %all-gather.12.cloned.1.call-start = ((), (), s32[]{:S(2)}) async-start(), calls=%async_computation.8 | async-start | bytes 1310720 | tf_op jit(solution)/shard_map/while/body/eval_jaxpr/all_gather | solution.py:63
  1829.8 82.9 %all-gather.10.cloned.1.call-start = ((), (), s32[]{:S(2)}) async-start(), calls=%async_computation.6 | async-start | bytes 5242880 | tf_op jit(solution)/shard_map/all_gather | solution.py:94
  1830.8 240.1 %all-gather.8.cloned.1.call-start = ((), (), s32[]{:S(2)}) async-start(), calls=%async_computation.5 | async-start | bytes 20971520 | tf_op jit(solution)/shard_map/all_gather | solution.py:95
  (18 other events, 5451.5 us)
Sparse Core Ops, SparseCore 0:
  44.6 27.6 reduce-scatter.2
  74.6 181.5 reduce-scatter.4
  270.0 36.7 all-reduce.1
  368.6 35.5 all-reduce.1
  406.0 26.3 all-gather.11
  466.4 35.5 all-reduce.1
  503.9 26.3 all-gather.11
  564.0 35.5 all-reduce.1
  601.5 26.3 all-gather.11
  661.6 35.5 all-reduce.1
  699.1 26.3 all-gather.11
  759.2 35.5 all-reduce.1
  856.6 35.5 all-reduce.1
  954.0 35.5 all-reduce.1
  1051.6 35.5 all-reduce.1
  1149.5 35.5 all-reduce.1
  1247.1 35.5 all-reduce.1
  1344.7 35.5 all-reduce.1
  1442.4 35.5 all-reduce.1
  1540.0 35.5 all-reduce.1
  1637.9 35.5 all-reduce.1
  1735.6 35.5 all-reduce.1
  1831.9 80.7 all-gather.9
  1914.3 156.5 all-gather.7
  (13 shorter events, 324.2 us)
where the time goes:
time: 2400 us; the launch traced here: 2390 us
  waiting for transfers between devices  1460 us (61%)
  other arithmetic  584 us (24%)
  matrix products  154 us (6%)
  local copies, waits for them, and re-layouts  131 us (5%)
  blocking collectives  39.8 us (2%)
    psum x16, waiting for transfers between devices, from_root(): return lax.psum(block, axis)  598 us
    all_gather x16, waiting for transfers between devices, factor_step(): lax.all_gather(row_raw, 'gx', axis=0, tiled=True)  449 us
    another operation x48, other arithmetic, factor_step(): chol = jnp.linalg.cholesky(own_diag)  199 us
    reduce_scatter x1, waiting for transfers between devices, on_device(): lax.psum_scatter(halves, ('gx', 'gy'), scatter_dimension=0, tiled=True)  183 us
    another operation x3, other arithmetic, on_device(): jax.scipy.linalg.solve_triangular(lower, middle, lower=True, trans=1)  170 us
    another operation x32, other arithmetic, factor_step(): solved = jax.scipy.linalg.solve_triangular(chol, stacked, lower=True)  168 us
    all_gather x1, waiting for transfers between devices, on_device(): whole = lax.all_gather(across, 'gx', axis=0, tiled=True)  112 us
    all_gather x1, waiting for transfers between devices, on_device(): across = lax.all_gather(shaped, 'gy', axis=3, tiled=True)  81.8 us
  transfers between devices with their start and end apart: 37, of which 37 were waited for; matrix products, arithmetic and copies ran while one was open for 0% of the time, Pallas kernels for 0%

commit v1 on v0

--- a/solution.py
+++ b/solution.py
@@ -9,7 +9,7 @@
 
 def from_root(block, axis, source):
     block = jnp.where(lax.axis_index(axis) == source, block, jnp.zeros_like(block))
-    return lax.psum(block, axis)
+    return jnp.sum(lax.all_gather(block, axis), axis=0)
 
 
 def on_device(blocks, coefficients, residuals):

time: 2400 us -> 2270 us (0.946)
  waiting for transfers between devices: 1460 us -> 1300 us
  other arithmetic: 584 us -> 614 us
    psum x16 -> x0, waiting for transfers between devices: 598 us -> none  [from_root(): return lax.psum(block, axis)]
    all_gather x0 -> x16, waiting for transfers between devices: none -> 464 us  [from_root(): return jnp.sum(lax.all_gather(block, axis), axis=0)]
    reduce_sum x0 -> x16, other arithmetic: none -> 32.1 us  [from_root(): return jnp.sum(lax.all_gather(block, axis), axis=0)]
    all_gather x16, waiting for transfers between devices: 449 us -> 419 us  [factor_step(): lax.all_gather(row_raw, 'gx', axis=0, tiled=True)]
where the time goes in v1:
time: 2270 us; the launch traced here: 2260 us
  waiting for transfers between devices  1300 us (57%)
  other arithmetic  614 us (27%)
  matrix products  154 us (7%)
  local copies, waits for them, and re-layouts  129 us (6%)
  blocking collectives  39.8 us (2%)
    all_gather x16, waiting for transfers between devices, from_root(): return jnp.sum(lax.all_gather(block, axis), axis=0)  464 us
    all_gather x16, waiting for transfers between devices, factor_step(): lax.all_gather(row_raw, 'gx', axis=0, tiled=True)  419 us
    another operation x48, other arithmetic, factor_step(): chol = jnp.linalg.cholesky(own_diag)  198 us
    reduce_scatter x1, waiting for transfers between devices, on_device(): lax.psum_scatter(halves, ('gx', 'gy'), scatter_dimension=0, tiled=True)  183 us
    another operation x3, other arithmetic, on_device(): jax.scipy.linalg.solve_triangular(lower, middle, lower=True, trans=1)  170 us
    another operation x32, other arithmetic, factor_step(): solved = jax.scipy.linalg.solve_triangular(chol, stacked, lower=True)  167 us
    all_gather x1, waiting for transfers between devices, on_device(): whole = lax.all_gather(across, 'gx', axis=0, tiled=True)  112 us
    all_gather x1, waiting for transfers between devices, on_device(): across = lax.all_gather(shaped, 'gy', axis=3, tiled=True)  81.8 us
  transfers between devices with their start and end apart: 37, of which 37 were waited for; matrix products, arithmetic and copies ran while one was open for 0% of the time, Pallas kernels for 0%

profile of v1, /device:TPU:0, one launch (start us, length us, event | category | flops | bytes accessed | tf_op | source)
XLA Modules:
  0.0 2255.4 jit_solution(14142873615673086542)
XLA Ops:
  44.6 27.8 %reduce-scatter.3.cloned.1.call-done = f32[16,4,64,4,128]{4,2,3,1,0:T(8,128)} async-done(((f32[16,4,128,4,128]{4,2,3,1,0:T(8,128)}), f32[16,4,64,4,128]{4,2,3,1,0:T(8,128)}) %reduce-scatter.3.cloned.1.call-update) | async-done | bytes 8388624 | tf_op jit(solution)/shard_map/reduce_scatter | solution.py:43
  72.9 183.3 %reduce-scatter.5.cloned.1.call-done = f32[1,4,64,4,128]{4,2,3,1,0:T(8,128)} async-done(((f32[16,4,64,4,128]{4,2,3,1,0:T(8,128)}), f32[1,4,64,4,128]{4,2,3,1,0:T(8,128)}) %reduce-scatter.5.cloned.1.call-update) | async-done | bytes 524304 | tf_op jit(solution)/shard_map/reduce_scatter | solution.py:44
  266.6 1428.6 %while.20 = (s32[]{:T(128)}, f32[4,128,4,128]{3,1,2,0:T(8,128)}, f32[4,128,4,128]{3,1,2,0:T(8,128)S(1)}, s32[]{:T(128)}, s32[]{:T(128)}, /*index=5*/s32[]{:T(128...) while((s32[]{:T(128)}, f32[4,128,4,128]{3,1,2,0:T(8,128)}, ...), condition=%wide.region_6.7_spmd.clone, body=%wide.region_2.6_spmd.clone.sunk | while | flops 806437056 | bytes 16058448 | solution.py:92
  268.5 29.9 %all-gather.17.cloned.1.call-done = f32[16,128,1,128]{3,1,2,0:T(8,128)} async-done(((f32[4,128,1,128]{3,1,2,0:T(8,128)}), f32[16,128,1,128]{3,1,2,0:T(8,128)}) %all-gather.17.cloned.1.call-update) | async-done | bytes 1048592 | tf_op jit(solution)/shard_map/while/body/eval_jaxpr/all_gather | solution.py:12
  358.6 28.8 %all-gather.17.cloned.1.call-done = f32[16,128,1,128]{3,1,2,0:T(8,128)} async-done(((f32[4,128,1,128]{3,1,2,0:T(8,128)}), f32[16,128,1,128]{3,1,2,0:T(8,128)}) %all-gather.17.cloned.1.call-update) | async-done | bytes 1048592 | tf_op jit(solution)/shard_map/while/body/eval_jaxpr/all_gather | solution.py:12
  447.7 29.1 %all-gather.17.cloned.1.call-done = f32[16,128,1,128]{3,1,2,0:T(8,128)} async-done(((f32[4,128,1,128]{3,1,2,0:T(8,128)}), f32[16,128,1,128]{3,1,2,0:T(8,128)}) %all-gather.17.cloned.1.call-update) | async-done | bytes 1048592 | tf_op jit(solution)/shard_map/while/body/eval_jaxpr/all_gather | solution.py:12
  537.2 28.8 %all-gather.17.cloned.1.call-done = f32[16,128,1,128]{3,1,2,0:T(8,128)} async-done(((f32[4,128,1,128]{3,1,2,0:T(8,128)}), f32[16,128,1,128]{3,1,2,0:T(8,128)}) %all-gather.17.cloned.1.call-update) | async-done | bytes 1048592 | tf_op jit(solution)/shard_map/while/body/eval_jaxpr/all_gather | solution.py:12
  626.4 28.8 %all-gather.17.cloned.1.call-done = f32[16,128,1,128]{3,1,2,0:T(8,128)} async-done(((f32[4,128,1,128]{3,1,2,0:T(8,128)}), f32[16,128,1,128]{3,1,2,0:T(8,128)}) %all-gather.17.cloned.1.call-update) | async-done | bytes 1048592 | tf_op jit(solution)/shard_map/while/body/eval_jaxpr/all_gather | solution.py:12
  715.6 28.8 %all-gather.17.cloned.1.call-done = f32[16,128,1,128]{3,1,2,0:T(8,128)} async-done(((f32[4,128,1,128]{3,1,2,0:T(8,128)}), f32[16,128,1,128]{3,1,2,0:T(8,128)}) %all-gather.17.cloned.1.call-update) | async-done | bytes 1048592 | tf_op jit(solution)/shard_map/while/body/eval_jaxpr/all_gather | solution.py:12
  804.6 28.8 %all-gather.17.cloned.1.call-done = f32[16,128,1,128]{3,1,2,0:T(8,128)} async-done(((f32[4,128,1,128]{3,1,2,0:T(8,128)}), f32[16,128,1,128]{3,1,2,0:T(8,128)}) %all-gather.17.cloned.1.call-update) | async-done | bytes 1048592 | tf_op jit(solution)/shard_map/while/body/eval_jaxpr/all_gather | solution.py:12
  893.6 28.8 %all-gather.17.cloned.1.call-done = f32[16,128,1,128]{3,1,2,0:T(8,128)} async-done(((f32[4,128,1,128]{3,1,2,0:T(8,128)}), f32[16,128,1,128]{3,1,2,0:T(8,128)}) %all-gather.17.cloned.1.call-update) | async-done | bytes 1048592 | tf_op jit(solution)/shard_map/while/body/eval_jaxpr/all_gather | solution.py:12
  982.7 28.8 %all-gather.17.cloned.1.call-done = f32[16,128,1,128]{3,1,2,0:T(8,128)} async-done(((f32[4,128,1,128]{3,1,2,0:T(8,128)}), f32[16,128,1,128]{3,1,2,0:T(8,128)}) %all-gather.17.cloned.1.call-update) | async-done | bytes 1048592 | tf_op jit(solution)/shard_map/while/body/eval_jaxpr/all_gather | solution.py:12
  1071.9 29.1 %all-gather.17.cloned.1.call-done = f32[16,128,1,128]{3,1,2,0:T(8,128)} async-done(((f32[4,128,1,128]{3,1,2,0:T(8,128)}), f32[16,128,1,128]{3,1,2,0:T(8,128)}) %all-gather.17.cloned.1.call-update) | async-done | bytes 1048592 | tf_op jit(solution)/shard_map/while/body/eval_jaxpr/all_gather | solution.py:12
  1161.4 28.8 %all-gather.17.cloned.1.call-done = f32[16,128,1,128]{3,1,2,0:T(8,128)} async-done(((f32[4,128,1,128]{3,1,2,0:T(8,128)}), f32[16,128,1,128]{3,1,2,0:T(8,128)}) %all-gather.17.cloned.1.call-update) | async-done | bytes 1048592 | tf_op jit(solution)/shard_map/while/body/eval_jaxpr/all_gather | solution.py:12
  1250.6 28.8 %all-gather.17.cloned.1.call-done = f32[16,128,1,128]{3,1,2,0:T(8,128)} async-done(((f32[4,128,1,128]{3,1,2,0:T(8,128)}), f32[16,128,1,128]{3,1,2,0:T(8,128)}) %all-gather.17.cloned.1.call-update) | async-done | bytes 1048592 | tf_op jit(solution)/shard_map/while/body/eval_jaxpr/all_gather | solution.py:12
  1339.6 29.2 %all-gather.17.cloned.1.call-done = f32[16,128,1,128]{3,1,2,0:T(8,128)} async-done(((f32[4,128,1,128]{3,1,2,0:T(8,128)}), f32[16,128,1,128]{3,1,2,0:T(8,128)}) %all-gather.17.cloned.1.call-update) | async-done | bytes 1048592 | tf_op jit(solution)/shard_map/while/body/eval_jaxpr/all_gather | solution.py:12
  1429.1 28.8 %all-gather.17.cloned.1.call-done = f32[16,128,1,128]{3,1,2,0:T(8,128)} async-done(((f32[4,128,1,128]{3,1,2,0:T(8,128)}), f32[16,128,1,128]{3,1,2,0:T(8,128)}) %all-gather.17.cloned.1.call-update) | async-done | bytes 1048592 | tf_op jit(solution)/shard_map/while/body/eval_jaxpr/all_gather | solution.py:12
  1518.2 29.1 %all-gather.17.cloned.1.call-done = f32[16,128,1,128]{3,1,2,0:T(8,128)} async-done(((f32[4,128,1,128]{3,1,2,0:T(8,128)}), f32[16,128,1,128]{3,1,2,0:T(8,128)}) %all-gather.17.cloned.1.call-update) | async-done | bytes 1048592 | tf_op jit(solution)/shard_map/while/body/eval_jaxpr/all_gather | solution.py:12
  1607.6 29.1 %all-gather.17.cloned.1.call-done = f32[16,128,1,128]{3,1,2,0:T(8,128)} async-done(((f32[4,128,1,128]{3,1,2,0:T(8,128)}), f32[16,128,1,128]{3,1,2,0:T(8,128)}) %all-gather.17.cloned.1.call-update) | async-done | bytes 1048592 | tf_op jit(solution)/shard_map/while/body/eval_jaxpr/all_gather | solution.py:12
  1696.3 81.8 %all-gather.15.cloned.1.call-done = f32[4,128,16,128]{3,1,2,0:T(8,128)} async-done(((f32[4,128,4,128]{3,1,2,0:T(8,128)}), f32[4,128,16,128]{3,1,2,0:T(8,128)}) %all-gather.15.cloned.1.call-update) | async-done | bytes 4194320 | tf_op jit(solution)/shard_map/all_gather | solution.py:94
  1781.9 39.8 %psum.7 = f32[16,128]{1,0:T(8,128)S(1)} all-reduce(f32[16,128]{1,0:T(8,128)S(1)} %fusion.19), channel_id=1, replica_groups=mesh['gx'=4,'gy'=4,'gz'=2] {'gx','gy','gz'}, use_global_device_ids=true, to_apply=%region_7.8 | all-reduce | flops 2048 | bytes 16384 | tf_op jit(solution)/shard_map/psum | solution.py:38
  1824.6 111.7 %all-gather.13.cloned.1.call-done = f32[4,4,128,4,4,128]{5,2,4,3,1,0:T(8,128)} async-done(((f32[1,4,128,4,4,128]{5,2,4,3,1,0:T(8,128)}), f32[4,4,128,4,4,128]{5,2,4,3,1,0:T(8,128)}) %all-gather.13.cloned.1.call-update) | async-done | bytes 16777232 | tf_op jit(solution)/shard_map/all_gather | solution.py:95
  1989.6 47.6 %while.19 = (s32[]{:T(128)}, f32[2048,2048]{1,0:T(8,128)}, s32[16,2]{0,1:T(2,128)S(1)}, f32[16,128,128]{2,1,0:T(8,128)S(1)}, s32[]{:T(128)}) while((s32[]{:T(128)}, f32[2048,2048]{1,0:T(8,128)}, s32[16,2]{0,1:T(2,128)S(1)}, f32[16,128,128]{2,1,0:T(8,128)S(1)}, s32[]{:T(128)}) %tuple.184), condition=%wide.while_cond, body=%wide.while_body.sunk | while | flops 2 | bytes 131181 | solution.py:98
  2037.2 157.4 %custom-call.28 = f32[16,128,128]{1,2,0:T(8,128)S(1)} custom-call(f32[16,128,128]{2,1,0:T(8,128)S(1)} %get-tuple-element.183), custom_call_target="InvertDiagBlocksLowerTriangular" | custom-call | tf_op jit(solution)/shard_map/jit(_solve_triangular)/triangular_solve | solution.py:98
  (583 shorter events, 1172.2 us)
Async XLA Ops:
  7.2 65.2 %reduce-scatter.3.cloned.1.call-start = ((), (), s32[]{:S(2)}) async-start(), calls=%async_computation.2 | async-start | bytes 25165824 | tf_op jit(solution)/shard_map/reduce_scatter | solution.py:43
  44.5 211.7 %reduce-scatter.5.cloned.1.call-start = ((), (), s32[]{:S(2)}) async-start(), calls=%async_computation.3 | async-start | bytes 8912896 | tf_op jit(solution)/shard_map/reduce_scatter | solution.py:44
  72.4 194.0 %all-gather.11.cloned.1.call-start = ((), (), s32[]{:S(2)}) async-start(), calls=%async_computation.4 | async-start | bytes 1572864 | tf_op jit(solution)/shard_map/all_gather | solution.py:45
  266.6 31.8 %all-gather.17.cloned.1.call-start = ((), (), s32[]{:S(2)}) async-start(), calls=%async_computation.7 | async-start | bytes 1310720 | tf_op jit(solution)/shard_map/while/body/eval_jaxpr/all_gather | solution.py:12
  268.4 58.2 %all-gather.19.cloned.1.call-start = ((), (), s32[]{:S(2)}) async-start(), calls=%async_computation.8 | async-start | bytes 1310720 | tf_op jit(solution)/shard_map/while/body/eval_jaxpr/all_gather | solution.py:63
  358.5 57.2 %all-gather.19.cloned.1.call-start = ((), (), s32[]{:S(2)}) async-start(), calls=%async_computation.8 | async-start | bytes 1310720 | tf_op jit(solution)/shard_map/while/body/eval_jaxpr/all_gather | solution.py:63
  447.7 57.5 %all-gather.19.cloned.1.call-start = ((), (), s32[]{:S(2)}) async-start(), calls=%async_computation.8 | async-start | bytes 1310720 | tf_op jit(solution)/shard_map/while/body/eval_jaxpr/all_gather | solution.py:63
  537.2 57.2 %all-gather.19.cloned.1.call-start = ((), (), s32[]{:S(2)}) async-start(), calls=%async_computation.8 | async-start | bytes 1310720 | tf_op jit(solution)/shard_map/while/body/eval_jaxpr/all_gather | solution.py:63
  626.3 57.2 %all-gather.19.cloned.1.call-start = ((), (), s32[]{:S(2)}) async-start(), calls=%async_computation.8 | async-start | bytes 1310720 | tf_op jit(solution)/shard_map/while/body/eval_jaxpr/all_gather | solution.py:63
  715.5 57.0 %all-gather.19.cloned.1.call-start = ((), (), s32[]{:S(2)}) async-start(), calls=%async_computation.8 | async-start | bytes 1310720 | tf_op jit(solution)/shard_map/while/body/eval_jaxpr/all_gather | solution.py:63
  804.5 57.0 %all-gather.19.cloned.1.call-start = ((), (), s32[]{:S(2)}) async-start(), calls=%async_computation.8 | async-start | bytes 1310720 | tf_op jit(solution)/shard_map/while/body/eval_jaxpr/all_gather | solution.py:63
  893.5 57.2 %all-gather.19.cloned.1.call-start = ((), (), s32[]{:S(2)}) async-start(), calls=%async_computation.8 | async-start | bytes 1310720 | tf_op jit(solution)/shard_map/while/body/eval_jaxpr/all_gather | solution.py:63
  982.7 57.2 %all-gather.19.cloned.1.call-start = ((), (), s32[]{:S(2)}) async-start(), calls=%async_computation.8 | async-start | bytes 1310720 | tf_op jit(solution)/shard_map/while/body/eval_jaxpr/all_gather | solution.py:63
  1070.1 31.0 %all-gather.17.cloned.1.call-start = ((), (), s32[]{:S(2)}) async-start(), calls=%async_computation.7 | async-start | bytes 1310720 | tf_op jit(solution)/shard_map/while/body/eval_jaxpr/all_gather | solution.py:12
  1071.9 57.5 %all-gather.19.cloned.1.call-start = ((), (), s32[]{:S(2)}) async-start(), calls=%async_computation.8 | async-start | bytes 1310720 | tf_op jit(solution)/shard_map/while/body/eval_jaxpr/all_gather | solution.py:63
  1161.4 57.2 %all-gather.19.cloned.1.call-start = ((), (), s32[]{:S(2)}) async-start(), calls=%async_computation.8 | async-start | bytes 1310720 | tf_op jit(solution)/shard_map/while/body/eval_jaxpr/all_gather | solution.py:63
  1250.5 57.0 %all-gather.19.cloned.1.call-start = ((), (), s32[]{:S(2)}) async-start(), calls=%async_computation.8 | async-start | bytes 1310720 | tf_op jit(solution)/shard_map/while/body/eval_jaxpr/all_gather | solution.py:63
  1337.7 31.0 %all-gather.17.cloned.1.call-start = ((), (), s32[]{:S(2)}) async-start(), calls=%async_computation.7 | async-start | bytes 1310720 | tf_op jit(solution)/shard_map/while/body/eval_jaxpr/all_gather | solution.py:12
  1339.5 57.5 %all-gather.19.cloned.1.call-start = ((), (), s32[]{:S(2)}) async-start(), calls=%async_computation.8 | async-start | bytes 1310720 | tf_op jit(solution)/shard_map/while/body/eval_jaxpr/all_gather | solution.py:63
  1429.0 57.2 %all-gather.19.cloned.1.call-start = ((), (), s32[]{:S(2)}) async-start(), calls=%async_computation.8 | async-start | bytes 1310720 | tf_op jit(solution)/shard_map/while/body/eval_jaxpr/all_gather | solution.py:63
  1518.2 57.4 %all-gather.19.cloned.1.call-start = ((), (), s32[]{:S(2)}) async-start(), calls=%async_computation.8 | async-start | bytes 1310720 | tf_op jit(solution)/shard_map/while/body/eval_jaxpr/all_gather | solution.py:63
  1607.5 57.5 %all-gather.19.cloned.1.call-start = ((), (), s32[]{:S(2)}) async-start(), calls=%async_computation.8 | async-start | bytes 1310720 | tf_op jit(solution)/shard_map/while/body/eval_jaxpr/all_gather | solution.py:63
  1695.2 82.8 %all-gather.15.cloned.1.call-start = ((), (), s32[]{:S(2)}) async-start(), calls=%async_computation.6 | async-start | bytes 5242880 | tf_op jit(solution)/shard_map/all_gather | solution.py:94
  1696.2 240.1 %all-gather.13.cloned.1.call-start = ((), (), s32[]{:S(2)}) async-start(), calls=%async_computation.5 | async-start | bytes 20971520 | tf_op jit(solution)/shard_map/all_gather | solution.py:95
  (18 other events, 4938.8 us)
Sparse Core Ops, SparseCore 0:
  44.6 27.6 reduce-scatter.2
  74.6 181.5 reduce-scatter.4
  269.2 29.1 all-gather.16
  300.7 25.8 all-gather.18
  359.4 27.9 all-gather.16
  448.9 27.9 all-gather.16
  479.3 25.8 all-gather.18
  538.0 27.9 all-gather.16
  627.2 27.9 all-gather.16
  716.4 27.9 all-gather.16
  746.6 25.8 all-gather.18
  805.4 27.9 all-gather.16
  835.7 25.8 all-gather.18
  894.4 27.9 all-gather.16
  983.6 27.9 all-gather.16
  1073.0 27.9 all-gather.16
  1162.2 27.9 all-gather.16
  1251.4 27.9 all-gather.16
  1340.7 27.9 all-gather.16
  1429.9 27.9 all-gather.16
  1519.4 27.9 all-gather.16
  1608.7 27.9 all-gather.16
  1697.3 80.7 all-gather.14
  1779.7 156.5 all-gather.12
  (13 shorter events, 318.3 us)
